TPU v7x, 32 devices: a whole 2x2x4 slice. The times are simulated.
32 devices in a mesh: swath: 2 (over x), band: 16 (over z, y, core).
Axes of the slice: x: 2, y: 2, z: 4, core: 2. Of those that a mesh axis runs over, the one named last changes fastest.
Arguments:
- design: bfloat16 [512, 16384], P(('swath', 'band')), parts along dimension 0, may hold values from 0 to 1
- row_taps: bfloat16 [8, 33], replicated, may hold values from -1 to 1
- column_taps: bfloat16 [8, 33], replicated, may hold values from -1 to 1
- kernel_weight: float32 [8], replicated, may hold values from 0.5 to 2
- interp: bfloat16 [32, 8], replicated, may hold values from 0 to 0.29882812
- block_shift: int32 [2, 4, 16], P(None, 'swath', 'band'), parts along dimension 1, may hold values from -24 to 24
- block_phase: int32 [2, 4, 16], P(None, 'swath', 'band'), parts along dimension 1, may hold values from 0 to 31
- care: int32 [4, 16], P('swath', 'band'), parts along dimension 0, may hold values 0 or 1
- image: bfloat16 [512, 16384], P('swath', 'band'), parts along dimension 0, may hold values from 0 to 20, as said below
Outputs:
- diff_map: bfloat16 [512, 16384], P('swath', 'band'), parts along dimension 0
There are 2 independent parts, one for each index of `swath`. A program takes and returns all parts, laid end to end along the dimension named above; an argument that names none is the same for every part. Nothing has to cross between parts.
Inputs may be any that keep to these rules, and one draw needn't show every extreme that they name: `image`: nonnegative intensities.
All inputs are finite; a program needn't handle non-finite values. No bound on the sum of `care` on one device may be relied on, other than what follows from the above.
Results may differ from a plain program's by a relative error of at most 0.0045.
Values may be sent and summed in bfloat16 or wider, within the bound.
A program may use at most 64 MiB of HBM per device.

v0:
```python
import functools

import jax
import jax.numpy as jnp
from jax import lax
from jax.experimental import pallas as pl
from jax.experimental.pallas import tpu as pltpu
from jax.sharding import PartitionSpec as P

NK = 8
KH = 16
IH = 4
BLK = 128
P_SIZE = 28
LANES = 128
EDGE = 32
PART = 32
GROUP = 4
REACH = 2 * KH + 1

epsilon = 1e-05
def pin(x):
    return pltpu.with_memory_space_constraint(x, pltpu.HBM)

F32 = jnp.float32
BF16 = jnp.bfloat16


def banded(offset, taps, shape):
    place = (
        lax.broadcasted_iota(jnp.int32, shape, 0)
        - lax.broadcasted_iota(jnp.int32, shape, 1)
        - offset
    )
    matrix = jnp.zeros(shape, F32)
    for tap, value in enumerate(taps):
        matrix = jnp.where(place == tap, value, matrix)
    return matrix


def banded_rows(offset, taps, shape):
    place = (
        lax.broadcasted_iota(jnp.int32, shape, 1)
        - lax.broadcasted_iota(jnp.int32, shape, 0)
        - offset
    )
    matrix = jnp.zeros(shape, F32)
    for tap, value in enumerate(taps):
        matrix = jnp.where(place == tap, value, matrix)
    return matrix


def kernel(
    n, height, width,
    weight_hbm, shift_hbm, phase_hbm, care_hbm,
    design_hbm, row_hbm, column_hbm, interp_hbm, image_hbm,
    filt, mean_ref, scale_ref,
    weight_ref, shift_ref, phase_ref, care_ref,
    design_ref, row_ref, column_ref, interp_ref,
    sendbuf, recv, image, row_mats, column_mats, taps, table, smooth, intensity,
    diff, partial_sums, stats_mine, stats_all,
    send_sem, recv_sem, stat_send, stat_recv, load_sem,
):
    me = lax.axis_index("band")
    rows = design_ref.shape[0]
    strip = width // n
    panels = strip // LANES
    wide = strip + LANES
    block_rows = GROUP * rows
    window = block_rows + 2 * KH
    steps = n // GROUP

    barrier = pltpu.get_barrier_semaphore()

    def greet(i, carry):
        peer = lax.rem(me + i, n)
        pl.semaphore_signal(
            barrier, inc=1, device_id={"band": peer}, device_id_type=pl.DeviceIdType.MESH
        )
        return carry

    lax.fori_loop(1, n, greet, 0)

    loads = [
        pltpu.make_async_copy(source, target, load_sem.at[i])
        for i, (source, target) in enumerate(
            [
                (design_hbm, design_ref),
                (row_hbm, row_ref),
                (column_hbm, column_ref),
                (interp_hbm, interp_ref),
                (weight_hbm, weight_ref),
                (shift_hbm, shift_ref),
                (phase_hbm, phase_ref),
                (care_hbm, care_ref),
                (image_hbm, image),
            ]
        )
    ]
    for load in loads:
        load.start()
    loads[0].wait()

    lane = lax.broadcasted_iota(jnp.int32, (rows, LANES), 1)
    low = lane < LANES // 2
    zero_panel = jnp.zeros((rows, LANES), BF16)
    for owner in range(n):
        start = owner * strip
        sendbuf[owner, :, :strip] = design_ref[:, start : start + strip]
        after = design_ref[:, start + strip : start + strip + LANES] if owner < n - 1 else zero_panel
        before = design_ref[:, start - LANES : start] if owner > 0 else zero_panel
        sendbuf[owner, :, strip:] = jnp.where(low, after, before)

    pl.semaphore_wait(barrier, n - 1)

    def copy_to(peer):
        return pltpu.make_async_remote_copy(
            src_ref=sendbuf.at[peer],
            dst_ref=recv.at[pl.ds(pl.multiple_of(KH + me * rows, rows), rows), :],
            send_sem=send_sem.at[peer],
            recv_sem=recv_sem.at[me],
            device_id={"band": peer},
            device_id_type=pl.DeviceIdType.MESH,
        )

    def copy_from(peer):
        return pltpu.make_async_remote_copy(
            src_ref=sendbuf.at[peer],
            dst_ref=recv.at[pl.ds(pl.multiple_of(KH + peer * rows, rows), rows), :],
            send_sem=send_sem.at[peer],
            recv_sem=recv_sem.at[peer],
            device_id={"band": peer},
            device_id_type=pl.DeviceIdType.MESH,
        )

    def send(i, carry):
        @pl.when(me + i < n)
        def _():
            copy_to(me + i).start()

        @pl.when(me - i >= 0)
        def _():
            copy_to(me - i).start()

        return carry

    lax.fori_loop(1, n, send, 0)

    recv[pl.ds(pl.multiple_of(KH + me * rows, rows), rows), :] = sendbuf[me]
    recv[:KH, :] = jnp.zeros((KH, wide), BF16)
    recv[KH + height :, :] = jnp.zeros((KH, wide), BF16)
    intensity[:EDGE, :] = jnp.zeros((EDGE, wide), BF16)
    intensity[EDGE + height :, :] = jnp.zeros((EDGE, wide), BF16)
    diff[:8, :] = jnp.zeros((8, strip), F32)
    diff[8 + height :, :] = jnp.zeros((8, strip), F32)

    for load in loads[1:-1]:
        load.wait()
    taps[:NK, :REACH] = row_ref[...].astype(F32)
    taps[NK:, :REACH] = column_ref[...].astype(F32)
    table[...] = interp_ref[...].astype(F32)
    phases = lax.broadcasted_iota(jnp.int32, table.shape, 1)

    def chosen(phase):
        row = jnp.sum(jnp.where(phases == phase, table[...], 0.0), axis=1, keepdims=True)
        return [row[t : t + 1] for t in range(2 * IH)]

    def build(k, carry):
        row_taps = [taps[pl.ds(k, 1), t : t + 1] for t in range(REACH)]
        row_mats[pl.ds(pl.multiple_of(k * block_rows, block_rows), block_rows), :] = banded_rows(
            0, row_taps, (block_rows, window)
        ).astype(BF16)
        column_taps = [taps[pl.ds(NK + k, 1), t : t + 1] for t in range(REACH)]
        column_mats[k] = banded(LANES - P_SIZE - KH, column_taps, (2 * LANES, LANES)).astype(BF16)
        return carry

    lax.fori_loop(0, NK, build, 0)

    rising = me < n // 2

    def arrived(place):
        band = jnp.where(rising, place, n - 1 - place)

        @pl.when(jnp.logical_and(place < n, band != me))
        def _():
            copy_from(band).wait_recv()

    first_column = me * strip - P_SIZE
    column = lax.broadcasted_iota(jnp.int32, (block_rows, LANES), 1)

    per_block = BLK // block_rows
    count = height // BLK
    part_rows = PART
    parts = BLK // part_rows

    def render(i, carry):
        for more in range(1, GROUP + 1):
            arrived(i * GROUP + more)
        group = jnp.where(rising, i, steps - 1 - i)
        start = pl.multiple_of(group * block_rows, block_rows)
        smooth[...] = jnp.dot(
            row_mats[...], recv[pl.ds(start, window), :], preferred_element_type=F32
        ).astype(BF16)
        total = jnp.zeros(((panels + 1) * block_rows, LANES), F32)
        for k in range(NK):
            own = smooth[k * block_rows : (k + 1) * block_rows, :]
            pieces = [jnp.concatenate([own[:, strip:], own[:, :LANES]], axis=1)]
            pieces += [own[:, (p - 1) * LANES : (p + 1) * LANES] for p in range(1, panels + 1)]
            field = jnp.dot(
                jnp.concatenate(pieces, axis=0), column_mats[k], preferred_element_type=F32
            )
            total = total + weight_ref[k] * field * field
        into = pl.multiple_of(EDGE + start, EDGE)
        for p in range(panels + 1):
            part = total[p * block_rows : (p + 1) * block_rows]
            if p in (0, panels):
                at = column + (first_column + p * LANES)
                part = jnp.where(jnp.logical_and(at >= 0, at < width), part, 0.0)
            intensity[pl.ds(into, block_rows), p * LANES : (p + 1) * LANES] = part.astype(BF16)

        @pl.when(jnp.logical_and(i >= per_block, lax.rem(i, per_block) == 0))
        def _():
            warp(i // per_block - 1)

        return carry

    def warp(place):
        b = jnp.where(rising, place, count - 1 - place)
        u = chosen(phase_ref[0, 0, b])
        v = chosen(phase_ref[1, 0, b])
        row_matrix = banded_rows(
            EDGE + 1 - IH + shift_ref[0, 0, b], u, (BLK, BLK + 2 * EDGE)
        ).astype(BF16)
        column_matrix = banded(
            P_SIZE + 1 - IH + shift_ref[1, 0, b], v, (2 * LANES, LANES)
        ).astype(BF16)
        start = pl.multiple_of(b * BLK, BLK)
        partial = jnp.dot(
            row_matrix, intensity[pl.ds(start, BLK + 2 * EDGE), :], preferred_element_type=F32
        ).astype(BF16)
        pieces = [partial[:, p * LANES : (p + 2) * LANES] for p in range(panels)]
        warped = jnp.dot(
            jnp.concatenate(pieces, axis=0), column_matrix, preferred_element_type=F32
        )
        care = care_ref[0, b].astype(F32)
        for p in range(panels):
            measured = image[pl.ds(start, BLK), p * LANES : (p + 1) * LANES].astype(F32)
            diff[pl.ds(pl.multiple_of(8 + start, 8), BLK), p * LANES : (p + 1) * LANES] = care * (
                measured - warped[p * BLK : (p + 1) * BLK]
            )

        first_part = place * parts - jnp.where(place > 0, 1, 0)
        last_part = (place + 1) * parts - jnp.where(place < count - 1, 1, 0)
        lax.fori_loop(first_part, last_part, stencil, 0)

    def stencil(place, carry):
        part = jnp.where(rising, place, count * parts - 1 - place)
        start = pl.multiple_of(part * part_rows, part_rows)
        around = diff[pl.ds(start, part_rows + 16), :]
        middle = around[8 : 8 + part_rows]
        value = middle + 0.5 * (around[7 : 7 + part_rows] + around[9 : 9 + part_rows])
        filt[pl.ds(start, part_rows), :] = value
        square = value * value
        first = partial_sums[:8, :]
        second = partial_sums[8:, :]
        for r in range(0, part_rows, 8):
            for p in range(panels):
                first = first + value[r : r + 8, p * LANES : (p + 1) * LANES]
                second = second + square[r : r + 8, p * LANES : (p + 1) * LANES]
        partial_sums[:8, :] = first
        partial_sums[8:, :] = second
        return carry

    loads[-1].wait()
    partial_sums[...] = jnp.zeros((16, LANES), F32)
    arrived(jnp.int32(0))
    lax.fori_loop(0, steps, render, 0)
    warp(jnp.int32(count - 1))
    stats_mine[0:1, :] = jnp.sum(partial_sums[:8, :], axis=0, keepdims=True)
    stats_mine[1:2, :] = jnp.sum(partial_sums[8:, :], axis=0, keepdims=True)

    def stat_to(peer):
        return pltpu.make_async_remote_copy(
            src_ref=stats_mine,
            dst_ref=stats_all.at[me],
            send_sem=stat_send.at[peer],
            recv_sem=stat_recv.at[me],
            device_id={"band": peer},
            device_id_type=pl.DeviceIdType.MESH,
        )

    def stat_from(peer):
        return pltpu.make_async_remote_copy(
            src_ref=stats_mine,
            dst_ref=stats_all.at[peer],
            send_sem=stat_send.at[peer],
            recv_sem=stat_recv.at[peer],
            device_id={"band": peer},
            device_id_type=pl.DeviceIdType.MESH,
        )

    def send_stats(i, carry):
        peer = lax.rem(me + n // 2 + i, n)

        @pl.when(peer != me)
        def _():
            stat_to(peer).start()

        return carry

    lax.fori_loop(0, n, send_stats, 0)
    stats_all[me] = stats_mine[...]

    def finish_sends(i, carry):
        peer = lax.rem(me + i, n)
        copy_to(peer).wait_send()
        return carry

    lax.fori_loop(1, n, finish_sends, 0)

    def take_stats(i, carry):
        peer = lax.rem(me + i, n)
        stat_from(peer).wait_recv()
        stat_to(peer).wait_send()
        return carry

    lax.fori_loop(1, n, take_stats, 0)

    sums = lax.fori_loop(
        0, n, lambda i, carry: carry + stats_all[i], jnp.zeros((2, LANES), F32)
    )
    cells = height * width
    mean = jnp.sum(sums[0:1], axis=1, keepdims=True) / cells
    power = jnp.sum(sums[1:2], axis=1, keepdims=True) / cells
    scale = lax.rsqrt(power - mean * mean + epsilon)
    mean_ref[...] = jnp.broadcast_to(mean, (1, strip))
    for b in range(count):
        scale_ref[b : b + 1, :] = jnp.broadcast_to(care_ref[0, b].astype(F32) * scale, (1, strip))


def on_device(
    design, row_taps, column_taps, kernel_weight, interp, block_shift, block_phase, care, image
):
    n = lax.axis_size("band")
    rows, width = design.shape
    height, strip = image.shape
    wide = strip + LANES
    block_rows = GROUP * rows
    window = block_rows + 2 * KH
    count = height // BLK
    hbm = pl.BlockSpec(memory_space=pltpu.HBM)
    vmem = pl.BlockSpec(memory_space=pltpu.VMEM)
    filtered, mean, scale = pl.pallas_call(
        functools.partial(kernel, n, height, width),
        out_shape=(
            jax.ShapeDtypeStruct((height, strip), F32),
            jax.ShapeDtypeStruct((1, strip), F32),
            jax.ShapeDtypeStruct((count, strip), F32),
        ),
        in_specs=[hbm] * 9,
        out_specs=(vmem, vmem, vmem),
        scratch_shapes=[
            pltpu.SMEM((NK,), F32),
            pltpu.SMEM((2, 1, count), jnp.int32),
            pltpu.SMEM((2, 1, count), jnp.int32),
            pltpu.SMEM((1, count), jnp.int32),
            pltpu.VMEM((rows, width), BF16),
            pltpu.VMEM(row_taps.shape, BF16),
            pltpu.VMEM(column_taps.shape, BF16),
            pltpu.VMEM(interp.shape[::-1], BF16),
            pltpu.VMEM((n, rows, wide), BF16),
            pltpu.VMEM((height + 2 * KH, wide), BF16),
            pltpu.VMEM((height, strip), BF16),
            pltpu.VMEM((NK * block_rows, window), BF16),
            pltpu.VMEM((NK, 2 * LANES, LANES), BF16),
            pltpu.VMEM((2 * NK, LANES), F32),
            pltpu.VMEM(interp.shape[::-1], F32),
            pltpu.VMEM((NK * block_rows, wide), BF16),
            pltpu.VMEM((height + 2 * EDGE, wide), BF16),
            pltpu.VMEM((height + 16, strip), F32),
            pltpu.VMEM((16, LANES), F32),
            pltpu.VMEM((2, LANES), F32),
            pltpu.VMEM((n, 2, LANES), F32),
            pltpu.SemaphoreType.DMA((n,)),
            pltpu.SemaphoreType.DMA((n,)),
            pltpu.SemaphoreType.DMA((n,)),
            pltpu.SemaphoreType.DMA((n,)),
            pltpu.SemaphoreType.DMA((9,)),
        ],
        compiler_params=pltpu.CompilerParams(
            collective_id=0, has_side_effects=True, vmem_limit_bytes=32 * 1024 * 1024
        ),
    )(
        pin(kernel_weight),
        pin(jnp.transpose(block_shift, (0, 2, 1))),
        pin(jnp.transpose(block_phase, (0, 2, 1))),
        pin(care.T),
        pin(design),
        pin(row_taps),
        pin(column_taps),
        pin(interp.T),
        pin(image),
    )
    blocks = filtered.reshape(count, BLK, strip)
    out = (blocks - mean[:, None]) * scale[:, None]
    return out.reshape(height, strip).astype(BF16)


def solution(mesh):
    placed = (
        P(("swath", "band"), None),
        P(),
        P(),
        P(),
        P(),
        P(None, "swath", "band"),
        P(None, "swath", "band"),
        P("swath", "band"),
        P("swath", "band"),
    )
    return jax.shard_map(
        on_device, mesh=mesh, in_specs=placed, out_specs=P("swath", "band"), check_vma=False
    )
```

profile of v0, /device:TPU:0, one launch (start us, length us, event | category | flops | bytes accessed | tf_op | source)
XLA Modules:
  0.0 30.8 jit_solution(14589962721495561539)
XLA Ops:
  0.0 29.8 %shard_map.91 = (f32[256,1024]{1,0:T(8,128)S(1)}, f32[1,1024]{1,0:T(1,128)S(1)}, f32[2,1024]{1,0:T(2,128)S(1)}) custom-call(f32[8]{0:T(128)} %weight_hbm.1, s32[2,1,2]{2,1,0:T(1,128)} %bitcast.15, s32[2,1,2]{2,1,0:T(1,128)} %bitcast.16, s32[1,2]{1,0:T(1,128)} %bitcast.17, bf16[16,16384]{1,0:T(8,128)(2,1)} %design_hbm.1, bf16[8,33]{1,0:T(8,128)(2,1)} %row_hbm.1, ...), custom_call_target="tpu_custom_call" | custom-call | tf_op jit(solution)/shard_map/pallas_call | solution.py:353
  29.8 0.9 %fusion = bf16[256,1024]{1,0:T(8,128)(2,1)} fusion(f32[256,1024]{1,0:T(8,128)S(1)} %get-tuple-element.8, f32[2,1024]{1,0:T(2,128)S(1)} %get-tuple-element.10, f32[1024]{0:T(1024)S(1)} %bitcast.13), kind=kLoop, calls=%fused_computation.1 | loop fusion | flops 786432 | bytes 1585152 | tf_op jit(solution)/shard_map/convert_element_type | solution.py:406
where the time goes:
time: 30.9 us; the launch traced here: 30.8 us
  Pallas kernels  29.8 us (96%)
  other arithmetic  0.92 us (3%)
    pallas_call x1, Pallas kernels, on_device(): pl.pallas_call(functools.partial(kernel, n, height, width), out_shape=(ja...  29.8 us
    convert_element_type x1, other arithmetic, on_device(): return out.reshape(height, strip).astype(BF16)  0.92 us

commit v1 on v0

v1 whole, which is shorter than its diff:
```python
import functools

import jax
import jax.numpy as jnp
from jax import lax
from jax.experimental import pallas as pl
from jax.experimental.pallas import tpu as pltpu
from jax.sharding import PartitionSpec as P

NK = 8
KH = 16
IH = 4
BLK = 128
P_SIZE = 28
LANES = 128
HALF = LANES // 2
EDGE = 32
UNIT = 128
LEVELS = 4
REACH = 2 * KH + 1
LEAD = P_SIZE + KH
INNER = LANES - LEAD

epsilon = 1e-05

F32 = jnp.float32
BF16 = jnp.bfloat16


def pin(x):
    return pltpu.with_memory_space_constraint(x, pltpu.HBM)


def skewed(row, rows):
    base = jnp.broadcast_to(row, (rows, row.shape[1]))
    return pltpu.roll(base, 0, 1, stride=1, stride_axis=0)


def split(total):
    return [min(UNIT, total - at) for at in range(0, total, UNIT)]


def plan(tiles):
    if tiles < 4:
        return [[(0, tiles)]]
    events = [[(0, 1), (tiles - 1, 1)]]
    low, high = 1, tiles - 2
    left = True
    while low <= high:
        span = min(2, high - low + 1)
        events.append([(low if left else high - span + 1, span)])
        low, high = (low + span, high) if left else (low, high - span)
        left = not left
    return events


def kernel(
    n, height, width,
    weight_hbm, shift_hbm, phase_hbm, care_hbm,
    design_hbm, row_hbm, column_hbm, interp_hbm, image_hbm,
    filt, mean_ref, scale_ref,
    weight_ref, shift_ref, phase_ref, care_ref,
    row_ref, column_ref, interp_ref,
    recv, before, after, ends, image, row_mats, column_mats, outer_mats,
    warp_rows, warp_columns, warp_last, smooth, intensity, partial,
    diff, partial_sums, stats_mine, stats_all,
    send_sem, recv_sem, relay_send, relay_recv, stat_send, stat_recv, load_sem,
):
    me = lax.axis_index("band")
    rows = height // n
    strip = width // n
    tiles = strip // LANES
    level_rows = height // LEVELS
    half_rows = 2 * level_rows
    count = height // BLK
    events = plan(tiles)
    pieces_of = [(e, lo, span) for e, event in enumerate(events) for lo, span in event]

    barrier = pltpu.get_barrier_semaphore()

    def greet(i, carry):
        peer = lax.rem(me + i, n)
        pl.semaphore_signal(
            barrier, inc=1, device_id={"band": peer}, device_id_type=pl.DeviceIdType.MESH
        )
        return carry

    lax.fori_loop(1, n, greet, 0)

    mine = pl.ds(pl.multiple_of(KH + me * rows, rows), rows)
    loads = [
        pltpu.make_async_copy(source, target, load_sem.at[i])
        for i, (source, target) in enumerate(
            [
                (row_hbm, row_ref),
                (column_hbm, column_ref),
                (interp_hbm, interp_ref),
                (weight_hbm, weight_ref),
                (shift_hbm, shift_ref),
                (phase_hbm, phase_ref),
                (care_hbm, care_ref),
                (image_hbm, image),
                (
                    design_hbm.at[:, pl.ds(pl.multiple_of(me * strip, LANES), strip)],
                    recv.at[mine, :],
                ),
            ]
        )
    ]
    for load in loads:
        load.start()

    flips = {}
    bit = 1
    while bit < n:
        flips[bit] = bit * (1 - 2 * lax.rem(me // bit, 2))
        bit *= 2

    def partner(i):
        return me + sum(flip for bit, flip in flips.items() if i & bit)

    def send(peer, slot, lo, span):
        pltpu.make_async_remote_copy(
            src_ref=design_hbm.at[
                :, pl.ds(pl.multiple_of(peer * strip + lo * LANES, LANES), span * LANES)
            ],
            dst_ref=recv.at[mine, pl.ds(lo * LANES, span * LANES)],
            send_sem=send_sem.at[slot],
            recv_sem=recv_sem.at[slot],
            device_id={"band": peer},
            device_id_type=pl.DeviceIdType.MESH,
        ).start()

    def block(extent, columns):
        return recv.at[pl.ds(0, extent), pl.ds(0, columns)]

    def settle(sem, extent, columns):
        pltpu.make_async_copy(block(extent, columns), block(extent, columns), sem).wait()

    sizes = [(half_rows - rows, strip), (level_rows, strip)] + [
        (level_rows, sum(span for _, span in event) * LANES) for event in events
    ]

    pl.semaphore_wait(barrier, n - 1)
    for i in range(1, n // 2):
        send(partner(i), 0, 0, tiles)
    for i in range(n // 2, 3 * n // 4):
        send(partner(i), 1, 0, tiles)
    for e, lo, span in pieces_of:
        for i in range(3 * n // 4, n):
            send(partner(i), 2 + e, lo, span)

    level = me // (n // LEVELS)
    second = lax.rem(level + 2, LEVELS)
    third = LEVELS - 1 - level
    upper = level // 2

    def by_level(*values):
        out = jnp.int32(values[0])
        for i in range(1, LEVELS):
            out = jnp.where(level == i, values[i], out)
        return pl.multiple_of(out, KH)

    first_rows = half_rows - KH
    second_rows = level_rows - KH
    third_rows = level_rows + 2 * KH
    first_start = by_level(0, 0, half_rows + KH, half_rows + KH)
    second_start = by_level(
        half_rows - KH, height - second_rows, 0, half_rows + KH - second_rows
    )
    third_start = by_level(
        height - third_rows, half_rows - KH, half_rows + KH - third_rows, 0
    )

    zero_rows = jnp.zeros((KH, LANES), BF16)
    for edge in (before, after):
        edge[:KH, :] = zero_rows
        edge[KH + height :, :] = zero_rows
    recv[:KH, :] = jnp.zeros((KH, strip), BF16)
    recv[KH + height :, :] = jnp.zeros((KH, strip), BF16)

    @pl.when(me == 0)
    def _():
        before[KH : KH + height, :] = jnp.zeros((height, LANES), BF16)

    @pl.when(me == n - 1)
    def _():
        after[KH : KH + height, :] = jnp.zeros((height, LANES), BF16)

    wide = strip + LANES
    intensity[:EDGE, :] = jnp.zeros((EDGE, wide), BF16)
    intensity[EDGE + height :, :] = jnp.zeros((EDGE, wide), BF16)
    diff[:8, :] = jnp.zeros((8, strip), F32)
    diff[8 + height :, :] = jnp.zeros((8, strip), F32)
    partial_sums[...] = jnp.zeros((16, LANES), F32)

    for load in loads[:-2]:
        load.wait()

    pad = jnp.zeros((NK, LANES - REACH), F32)
    row_table = jnp.concatenate([row_ref[...].astype(F32), pad, jnp.zeros((NK, LANES), F32)], axis=1)
    column_table = jnp.concatenate([column_ref[...].astype(F32), pad], axis=1)
    from_lane = lax.broadcasted_iota(jnp.int32, (LANES, LANES), 0)
    to_lane = lax.broadcasted_iota(jnp.int32, (LANES, LANES), 1)
    turned = jnp.where(lax.rem(2 * LANES - INNER - to_lane, LANES) == from_lane, 1.0, 0.0)
    backward = jnp.dot(
        column_table.astype(BF16), turned.astype(BF16), preferred_element_type=F32
    )
    backward_half = pltpu.roll(backward, HALF, 1)
    square = (2 * LANES, LANES)
    down = lax.broadcasted_iota(jnp.int32, square, 0)
    across = lax.broadcasted_iota(jnp.int32, square, 1)
    place = down - across - INNER
    inside = jnp.logical_and(place >= 0, place < REACH)
    low_lane = across < HALF
    place_far = lax.rem(down - across - INNER - HALF + 4 * LANES, 2 * LANES)
    inside_outer = jnp.where(low_lane, jnp.where(inside, 1, 0), jnp.where(place_far < REACH, 1, 0)) > 0
    for k in range(NK):
        row_mats[k * UNIT : (k + 1) * UNIT, :] = skewed(row_table[k : k + 1], UNIT).astype(BF16)
        near = skewed(backward[k : k + 1], 2 * LANES)
        far = skewed(backward_half[k : k + 1], 2 * LANES)
        column_mats[k] = jnp.where(inside, near, 0.0).astype(BF16)
        outer_mats[k] = jnp.where(
            inside_outer, jnp.where(low_lane, near, far), 0.0
        ).astype(BF16)

    table = interp_ref[...].astype(F32)
    phases = lax.broadcasted_iota(jnp.int32, table.shape, 1)
    lane_wide = lax.broadcasted_iota(jnp.int32, (1, 2 * LANES), 1)
    lane_one = lax.broadcasted_iota(jnp.int32, (1, LANES), 1)

    def chosen(phase):
        row = jnp.sum(jnp.where(phases == phase, table, 0.0), axis=1, keepdims=True)
        return [row[t : t + 1] for t in range(2 * IH)]

    for b in range(count):
        u = chosen(phase_ref[0, 0, b])
        v = chosen(phase_ref[1, 0, b])
        lead = EDGE + 1 - IH + shift_ref[0, 0, b]
        row = jnp.zeros((1, 2 * LANES), F32)
        for tap in range(2 * IH):
            row = jnp.where(lane_wide == lead + tap, u[tap], row)
        warp_rows[b] = skewed(row, BLK).astype(BF16)
        lead = P_SIZE + 1 - IH + shift_ref[1, 0, b]
        row = jnp.zeros((1, LANES), F32)
        for tap in range(2 * IH):
            row = jnp.where(lane_one == LANES - lead - tap, v[tap], row)
        steep = skewed(row, 2 * LANES)
        spot = down - across - lead
        matrix = jnp.where(jnp.logical_and(spot >= 0, spot < 2 * IH), steep, 0.0)
        warp_columns[b] = matrix.astype(BF16)
        warp_last[b, :LANES, :] = matrix[:LANES].astype(BF16)
        warp_last[b, LANES : LANES + HALF, :] = jnp.zeros((HALF, LANES), BF16)
        warp_last[b, LANES + HALF :, :] = matrix[LANES : LANES + HALF].astype(BF16)

    def relay(stage, peer, side, start, extent):
        span = pl.ds(pl.multiple_of(KH + start, KH), extent)
        source = recv.at[span, pl.ds(0, LANES)] if side == 0 else recv.at[
            span, pl.ds(strip - LANES, LANES)
        ]
        target = after.at[span, :] if side == 0 else before.at[span, :]
        return pltpu.make_async_remote_copy(
            src_ref=source,
            dst_ref=target,
            send_sem=relay_send.at[stage, side],
            recv_sem=relay_recv.at[stage, side],
            device_id={"band": peer},
            device_id_type=pl.DeviceIdType.MESH,
        )

    relays = [
        (upper * half_rows, half_rows),
        (second * level_rows, level_rows),
        (third * level_rows, level_rows),
    ]

    def pass_on(stage):
        @pl.when(me > 0)
        def _():
            relay(stage, me - 1, 0, *relays[stage]).start()

        @pl.when(me < n - 1)
        def _():
            relay(stage, me + 1, 1, *relays[stage]).start()

    def take_ends():
        for stage, (_, extent) in enumerate(relays):
            region = block(extent, LANES)

            @pl.when(me < n - 1)
            def _():
                pltpu.make_async_copy(region, region, relay_recv.at[stage, 0]).wait()

            @pl.when(me > 0)
            def _():
                pltpu.make_async_copy(region, region, relay_recv.at[stage, 1]).wait()

    def finish_relays():
        for stage, (_, extent) in enumerate(relays):
            region = block(extent, LANES)

            @pl.when(me > 0)
            def _():
                pltpu.make_async_copy(region, region, relay_send.at[stage, 0]).wait()

            @pl.when(me < n - 1)
            def _():
                pltpu.make_async_copy(region, region, relay_send.at[stage, 1]).wait()

    def row_kernels(extent):
        return jnp.concatenate(
            [row_mats[k * UNIT : k * UNIT + extent, : extent + 2 * KH] for k in range(NK)], axis=0
        )

    def smear(start, extent, at, lo, span):
        window = recv[
            pl.ds(pl.multiple_of(start, KH), extent + 2 * KH), lo * LANES : (lo + span) * LANES
        ]
        smooth[at : at + NK * extent, lo * LANES : (lo + span) * LANES] = jnp.dot(
            row_kernels(extent), window, preferred_element_type=F32
        ).astype(BF16)

    def render(start, extent, at, panels):
        into = pl.multiple_of(EDGE + start, KH)
        total = jnp.zeros((len(panels) * extent, LANES), F32)
        for k in range(NK):
            pieces = []
            for p in panels:
                own = pl.ds(at + k * extent, extent)
                if p == 0:
                    piece = smooth[own, :LANES]
                    pieces.append(jnp.concatenate([piece, piece], axis=1))
                else:
                    pieces.append(smooth[own, (p - 1) * LANES : (p + 1) * LANES])
            field = jnp.dot(
                jnp.concatenate(pieces, axis=0), column_mats[k], preferred_element_type=F32
            )
            total = total + weight_ref[k] * field * field
        for i, p in enumerate(panels):
            intensity[pl.ds(into, extent), p * LANES : (p + 1) * LANES] = total[
                i * extent : (i + 1) * extent
            ].astype(BF16)

    def render_outer():
        lane = lax.broadcasted_iota(jnp.int32, (height + 2 * KH, LANES), 1) < HALF
        ends[:, :LANES] = jnp.where(lane, after[...], before[...])
        ends[:, LANES:] = jnp.where(lane, recv[:, :LANES], recv[:, strip - LANES :])
        start = 0
        for extent in split(height):
            lanes = lax.broadcasted_iota(jnp.int32, (extent, LANES), 1)
            spread = jnp.dot(
                row_kernels(extent), ends[start : start + extent + 2 * KH, :],
                preferred_element_type=F32,
            ).astype(BF16)
            total = jnp.zeros((extent, LANES), F32)
            for k in range(NK):
                field = jnp.dot(
                    spread[k * extent : (k + 1) * extent], outer_mats[k],
                    preferred_element_type=F32,
                )
                total = total + weight_ref[k] * field * field
            left = lanes < HALF
            column = jnp.where(left, me * strip + lanes, me * strip + strip + lanes - HALF) - P_SIZE
            total = jnp.where(jnp.logical_and(column >= 0, column < width), total, 0.0).astype(BF16)
            into = slice(EDGE + start, EDGE + start + extent)
            intensity[into, strip:] = total
            intensity[into, :LANES] = jnp.where(lanes < LEAD, total, intensity[into, :LANES])
            start += extent

    def halfway(panels):
        runs = []
        for p in sorted(panels):
            if runs and runs[-1][1] == p:
                runs[-1][1] = p + 1
            else:
                runs.append([p, p + 1])
        for b in range(count):
            for lo, hi in runs:
                partial[b * BLK : (b + 1) * BLK, lo * LANES : hi * LANES] = jnp.dot(
                    warp_rows[b, :, : BLK + 2 * EDGE],
                    intensity[b * BLK : (b + 1) * BLK + 2 * EDGE, lo * LANES : hi * LANES],
                    preferred_element_type=F32,
                ).astype(BF16)

    def finish(targets):
        targets = sorted(targets)
        common = [q for q in targets if q < tiles - 1]
        for b in range(count):
            own = slice(b * BLK, (b + 1) * BLK)
            care = care_ref[0, b].astype(F32)
            results = []
            if common:
                warped = jnp.dot(
                    jnp.concatenate(
                        [partial[own, q * LANES : (q + 2) * LANES] for q in common], axis=0
                    ),
                    warp_columns[b],
                    preferred_element_type=F32,
                )
                results += [(q, warped[i * BLK : (i + 1) * BLK]) for i, q in enumerate(common)]
            if tiles - 1 in targets:
                q = tiles - 1
                results.append(
                    (
                        q,
                        jnp.dot(
                            partial[own, q * LANES : (q + 2) * LANES], warp_last[b],
                            preferred_element_type=F32,
                        ),
                    )
                )
            for q, warped in results:
                measured = image[own, q * LANES : (q + 1) * LANES].astype(F32)
                diff[8 + b * BLK : 8 + (b + 1) * BLK, q * LANES : (q + 1) * LANES] = care * (
                    measured - warped
                )
        first = partial_sums[:8, :]
        second = partial_sums[8:, :]
        for q in targets:
            column = slice(q * LANES, (q + 1) * LANES)
            for start in range(0, height, BLK):
                around = diff[start : start + BLK + 16, column]
                value = around[8 : 8 + BLK] + 0.5 * (around[7 : 7 + BLK] + around[9 : 9 + BLK])
                filt[start : start + BLK, column] = value
                power = value * value
                for r in range(0, BLK, 8):
                    first = first + value[r : r + 8]
                    second = second + power[r : r + 8]
        partial_sums[:8, :] = first
        partial_sums[8:, :] = second

    def whole(start, total):
        at = 0
        for extent in split(total):
            smear(start + at, extent, 0, 0, tiles)
            for p in range(0, tiles, 4):
                render(start + at, extent, 0, list(range(p, min(p + 4, tiles))))
            at += extent

    loads[-1].wait()
    settle(recv_sem.at[0], *sizes[0])
    pass_on(0)
    whole(first_start, first_rows)
    settle(recv_sem.at[1], *sizes[1])
    pass_on(1)
    whole(second_start, second_rows)
    loads[-2].wait()

    seen, drawn, halves, done = set(), set(), set(), set()
    for e, event in enumerate(events):
        settle(recv_sem.at[2 + e], *sizes[2 + e])
        if e == 0:
            pass_on(2)
        for lo, span in event:
            seen.update(range(lo, lo + span))
        fresh = [
            p for p in range(tiles)
            if p in seen and (p == 0 or p - 1 in seen) and p not in drawn
        ]
        drawn.update(fresh)
        at = 0
        for extent in split(third_rows):
            for lo, span in event:
                smear(third_start + at, extent, NK * at, lo, span)
            if fresh:
                render(third_start + at, extent, NK * at, fresh)
            at += extent
        if e == max(len(events) - 2, 0):
            take_ends()
            render_outer()
            drawn.add(tiles)
        if tiles in drawn:
            ready = drawn - halves
            halfway(ready)
            halves.update(ready)
            targets = {q for q in range(tiles) if q in halves and q + 1 in halves} - done
            finish(targets)
            done.update(targets)

    stats_mine[0:1, :] = jnp.sum(partial_sums[:8, :], axis=0, keepdims=True)
    stats_mine[1:2, :] = jnp.sum(partial_sums[8:, :], axis=0, keepdims=True)

    def stat_to(peer):
        return pltpu.make_async_remote_copy(
            src_ref=stats_mine,
            dst_ref=stats_all.at[me],
            send_sem=stat_send.at[peer],
            recv_sem=stat_recv.at[me],
            device_id={"band": peer},
            device_id_type=pl.DeviceIdType.MESH,
        )

    def stat_from(peer):
        return pltpu.make_async_remote_copy(
            src_ref=stats_mine,
            dst_ref=stats_all.at[peer],
            send_sem=stat_send.at[peer],
            recv_sem=stat_recv.at[peer],
            device_id={"band": peer},
            device_id_type=pl.DeviceIdType.MESH,
        )

    def send_stats(i, carry):
        peer = lax.rem(me + n // 2 + i, n)

        @pl.when(peer != me)
        def _():
            stat_to(peer).start()

        return carry

    lax.fori_loop(0, n, send_stats, 0)
    stats_all[me] = stats_mine[...]

    for slot, size in enumerate(sizes):
        settle(send_sem.at[slot], *size)
    finish_relays()

    def take_stats(i, carry):
        peer = lax.rem(me + i, n)
        stat_from(peer).wait_recv()
        stat_to(peer).wait_send()
        return carry

    lax.fori_loop(1, n, take_stats, 0)

    sums = lax.fori_loop(
        0, n, lambda i, carry: carry + stats_all[i], jnp.zeros((2, LANES), F32)
    )
    cells = height * width
    mean = jnp.sum(sums[0:1], axis=1, keepdims=True) / cells
    power = jnp.sum(sums[1:2], axis=1, keepdims=True) / cells
    scale = lax.rsqrt(power - mean * mean + epsilon)
    mean_ref[...] = jnp.broadcast_to(mean, (1, strip))
    for b in range(count):
        scale_ref[b : b + 1, :] = jnp.broadcast_to(care_ref[0, b].astype(F32) * scale, (1, strip))


def on_device(
    design, row_taps, column_taps, kernel_weight, interp, block_shift, block_phase, care, image
):
    n = lax.axis_size("band")
    rows, width = design.shape
    height, strip = image.shape
    wide = strip + LANES
    count = height // BLK
    slots = 2 + len(plan(strip // LANES))
    tall = height + 2 * KH
    hbm = pl.BlockSpec(memory_space=pltpu.HBM)
    vmem = pl.BlockSpec(memory_space=pltpu.VMEM)
    filtered, mean, scale = pl.pallas_call(
        functools.partial(kernel, n, height, width),
        out_shape=(
            jax.ShapeDtypeStruct((height, strip), F32),
            jax.ShapeDtypeStruct((1, strip), F32),
            jax.ShapeDtypeStruct((count, strip), F32),
        ),
        in_specs=[hbm] * 9,
        out_specs=(vmem, vmem, vmem),
        scratch_shapes=[
            pltpu.SMEM((NK,), F32),
            pltpu.SMEM((2, 1, count), jnp.int32),
            pltpu.SMEM((2, 1, count), jnp.int32),
            pltpu.SMEM((1, count), jnp.int32),
            pltpu.VMEM(row_taps.shape, BF16),
            pltpu.VMEM(column_taps.shape, BF16),
            pltpu.VMEM(interp.shape[::-1], BF16),
            pltpu.VMEM((tall, strip), BF16),
            pltpu.VMEM((tall, LANES), BF16),
            pltpu.VMEM((tall, LANES), BF16),
            pltpu.VMEM((tall, 2 * LANES), BF16),
            pltpu.VMEM((height, strip), BF16),
            pltpu.VMEM((NK * UNIT, 2 * LANES), BF16),
            pltpu.VMEM((NK, 2 * LANES, LANES), BF16),
            pltpu.VMEM((NK, 2 * LANES, LANES), BF16),
            pltpu.VMEM((count, BLK, 2 * LANES), BF16),
            pltpu.VMEM((count, 2 * LANES, LANES), BF16),
            pltpu.VMEM((count, 2 * LANES, LANES), BF16),
            pltpu.VMEM((NK * max(UNIT, height // LEVELS + 2 * KH), strip), BF16),
            pltpu.VMEM((height + 2 * EDGE, wide), BF16),
            pltpu.VMEM((height, wide), BF16),
            pltpu.VMEM((height + 16, strip), F32),
            pltpu.VMEM((16, LANES), F32),
            pltpu.VMEM((2, LANES), F32),
            pltpu.VMEM((n, 2, LANES), F32),
            pltpu.SemaphoreType.DMA((slots,)),
            pltpu.SemaphoreType.DMA((slots,)),
            pltpu.SemaphoreType.DMA((3, 2)),
            pltpu.SemaphoreType.DMA((3, 2)),
            pltpu.SemaphoreType.DMA((n,)),
            pltpu.SemaphoreType.DMA((n,)),
            pltpu.SemaphoreType.DMA((9,)),
        ],
        compiler_params=pltpu.CompilerParams(
            collective_id=0, has_side_effects=True, vmem_limit_bytes=48 * 1024 * 1024
        ),
    )(
        pin(kernel_weight),
        pin(jnp.transpose(block_shift, (0, 2, 1))),
        pin(jnp.transpose(block_phase, (0, 2, 1))),
        pin(care.T),
        pin(design),
        pin(row_taps),
        pin(column_taps),
        pin(interp.T),
        pin(image),
    )
    blocks = filtered.reshape(count, BLK, strip)
    out = (blocks - mean[:, None]) * scale[:, None]
    return out.reshape(height, strip).astype(BF16)


def solution(mesh):
    placed = (
        P(("swath", "band"), None),
        P(),
        P(),
        P(),
        P(),
        P(None, "swath", "band"),
        P(None, "swath", "band"),
        P("swath", "band"),
        P("swath", "band"),
    )
    return jax.shard_map(
        on_device, mesh=mesh, in_specs=placed, out_specs=P("swath", "band"), check_vma=False
    )
```

time: 30.9 us -> 28.6 us (0.926)
  Pallas kernels: 29.8 us -> 27.6 us
    pallas_call x1, Pallas kernels: 29.8 us -> 27.6 us  [on_device(): pl.pallas_call(functools.partial(kernel, n, height, width), out_shape=(ja...]
where the time goes in v1:
time: 28.6 us; the launch traced here: 28.5 us
  Pallas kernels  27.6 us (97%)
  other arithmetic  0.92 us (3%)
    pallas_call x1, Pallas kernels, on_device(): pl.pallas_call(functools.partial(kernel, n, height, width), out_shape=(ja...  27.6 us
    convert_element_type x1, other arithmetic, on_device(): return out.reshape(height, strip).astype(BF16)  0.92 us

profile of v1, /device:TPU:0, one launch (start us, length us, event | category | flops | bytes accessed | tf_op | source)
XLA Modules:
  0.0 28.5 jit_solution(9159803521473065962)
XLA Ops:
  0.0 27.6 %shard_map.91 = (f32[256,1024]{1,0:T(8,128)S(1)}, f32[1,1024]{1,0:T(1,128)S(1)}, f32[2,1024]{1,0:T(2,128)S(1)}) custom-call(f32[8]{0:T(128)} %weight_hbm.1, s32[2,1,2]{2,1,0:T(1,128)} %bitcast.15, s32[2,1,2]{2,1,0:T(1,128)} %bitcast.16, s32[1,2]{1,0:T(1,128)} %bitcast.17, bf16[16,16384]{1,0:T(8,128)(2,1)} %design_hbm.1, bf16[8,33]{1,0:T(8,128)(2,1)} %row_hbm.1, ...), custom_call_target="tpu_custom_call" | custom-call | tf_op jit(solution)/shard_map/pallas_call | solution.py:551
  27.6 0.9 %fusion = bf16[256,1024]{1,0:T(8,128)(2,1)} fusion(f32[256,1024]{1,0:T(8,128)S(1)} %get-tuple-element.8, f32[2,1024]{1,0:T(2,128)S(1)} %get-tuple-element.10, f32[1024]{0:T(1024)S(1)} %bitcast.13), kind=kLoop, calls=%fused_computation.1 | loop fusion | flops 786432 | bytes 1585152 | tf_op jit(solution)/shard_map/convert_element_type | solution.py:610

commit v2 on v1

--- a/solution.py
+++ b/solution.py
@@ -16,10 +16,13 @@
 HALF = LANES // 2
 EDGE = 32
 UNIT = 128
-LEVELS = 4
 REACH = 2 * KH + 1
 LEAD = P_SIZE + KH
 INNER = LANES - LEAD
+
+LEVELS = 4
+INNER_SENDS = {3: 0}
+OUTER_SENDS = {3: 0}
 
 epsilon = 1e-05
 
@@ -62,19 +65,17 @@
     weight_ref, shift_ref, phase_ref, care_ref,
     row_ref, column_ref, interp_ref,
     recv, before, after, ends, image, row_mats, column_mats, outer_mats,
-    warp_rows, warp_columns, warp_last, smooth, intensity, partial,
+    warp_rows, warp_columns, warp_last, crossed, intensity, partial,
     diff, partial_sums, stats_mine, stats_all,
-    send_sem, recv_sem, relay_send, relay_recv, stat_send, stat_recv, load_sem,
+    send_sem, recv_sem, relay_send, relay_recv, end_send, end_recv, end_load, stat_send, stat_recv, load_sem,
 ):
     me = lax.axis_index("band")
     rows = height // n
     strip = width // n
     tiles = strip // LANES
-    level_rows = height // LEVELS
-    half_rows = 2 * level_rows
+    tall = height + 2 * KH
     count = height // BLK
     events = plan(tiles)
-    pieces_of = [(e, lo, span) for e, event in enumerate(events) for lo, span in event]
 
     barrier = pltpu.get_barrier_semaphore()
 
@@ -131,46 +132,55 @@
             device_id_type=pl.DeviceIdType.MESH,
         ).start()
 
+    def send_ends():
+        for target, edge, tile in ((n // 2, before, -1), (n // 2 - 1, after, 0)):
+            source = design_hbm.at[:, pl.ds((n // 2) * strip + tile * LANES, LANES)]
+            place = edge.at[mine, :]
+
+            @pl.when(me != target)
+            def _():
+                pltpu.make_async_remote_copy(
+                    src_ref=source,
+                    dst_ref=place,
+                    send_sem=end_send.at[-tile],
+                    recv_sem=end_recv,
+                    device_id={"band": jnp.int32(target)},
+                    device_id_type=pl.DeviceIdType.MESH,
+                ).start()
+
+            @pl.when(me == target)
+            def _():
+                pltpu.make_async_copy(source, place, end_load).start()
+
     def block(extent, columns):
         return recv.at[pl.ds(0, extent), pl.ds(0, columns)]
 
     def settle(sem, extent, columns):
         pltpu.make_async_copy(block(extent, columns), block(extent, columns), sem).wait()
 
-    sizes = [(half_rows - rows, strip), (level_rows, strip)] + [
-        (level_rows, sum(span for _, span in event) * LANES) for event in events
-    ]
+    sizes = [(height - rows, sum(span for _, span in event) * LANES) for event in events]
 
     pl.semaphore_wait(barrier, n - 1)
-    for i in range(1, n // 2):
-        send(partner(i), 0, 0, tiles)
-    for i in range(n // 2, 3 * n // 4):
-        send(partner(i), 1, 0, tiles)
-    for e, lo, span in pieces_of:
-        for i in range(3 * n // 4, n):
-            send(partner(i), 2 + e, lo, span)
+
+    def send_pieces(chosen_events):
+        for e in chosen_events:
+            for i in range(1, n):
+                for lo, span in events[e]:
+                    send(partner(i), e, lo, span)
+
+    def send_after(e):
+        for mine_too, schedule in ((True, INNER_SENDS), (False, OUTER_SENDS)):
+            batch = [x for x in range(1, len(events)) if schedule.get(x, -1) == e]
+            if batch:
+                @pl.when(inner == mine_too)
+                def _():
+                    send_pieces(batch)
 
     level = me // (n // LEVELS)
-    second = lax.rem(level + 2, LEVELS)
-    third = LEVELS - 1 - level
-    upper = level // 2
-
-    def by_level(*values):
-        out = jnp.int32(values[0])
-        for i in range(1, LEVELS):
-            out = jnp.where(level == i, values[i], out)
-        return pl.multiple_of(out, KH)
-
-    first_rows = half_rows - KH
-    second_rows = level_rows - KH
-    third_rows = level_rows + 2 * KH
-    first_start = by_level(0, 0, half_rows + KH, half_rows + KH)
-    second_start = by_level(
-        half_rows - KH, height - second_rows, 0, half_rows + KH - second_rows
-    )
-    third_start = by_level(
-        height - third_rows, half_rows - KH, half_rows + KH - third_rows, 0
-    )
+    inner = jnp.logical_and(level > 0, level < LEVELS - 1)
+    send_pieces([0])
+    send_ends()
+    send_after(-1)
 
     zero_rows = jnp.zeros((KH, LANES), BF16)
     for edge in (before, after):
@@ -216,11 +226,12 @@
     place_far = lax.rem(down - across - INNER - HALF + 4 * LANES, 2 * LANES)
     inside_outer = jnp.where(low_lane, jnp.where(inside, 1, 0), jnp.where(place_far < REACH, 1, 0)) > 0
     for k in range(NK):
-        row_mats[k * UNIT : (k + 1) * UNIT, :] = skewed(row_table[k : k + 1], UNIT).astype(BF16)
+        row_mats[k] = skewed(row_table[k : k + 1], UNIT).astype(BF16)
         near = skewed(backward[k : k + 1], 2 * LANES)
         far = skewed(backward_half[k : k + 1], 2 * LANES)
-        column_mats[k] = jnp.where(inside, near, 0.0).astype(BF16)
-        outer_mats[k] = jnp.where(
+        half = slice((k % 2) * LANES, (k % 2 + 1) * LANES)
+        column_mats[k // 2, :, half] = jnp.where(inside, near, 0.0).astype(BF16)
+        outer_mats[k // 2, :, half] = jnp.where(
             inside_outer, jnp.where(low_lane, near, far), 0.0
         ).astype(BF16)
 
@@ -253,119 +264,121 @@
         warp_last[b, LANES : LANES + HALF, :] = jnp.zeros((HALF, LANES), BF16)
         warp_last[b, LANES + HALF :, :] = matrix[LANES : LANES + HALF].astype(BF16)
 
-    def relay(stage, peer, side, start, extent):
-        span = pl.ds(pl.multiple_of(KH + start, KH), extent)
-        source = recv.at[span, pl.ds(0, LANES)] if side == 0 else recv.at[
-            span, pl.ds(strip - LANES, LANES)
-        ]
+    def relay(peer, side):
+        span = pl.ds(KH, height)
+        source = recv.at[span, pl.ds(0 if side == 0 else strip - LANES, LANES)]
         target = after.at[span, :] if side == 0 else before.at[span, :]
         return pltpu.make_async_remote_copy(
             src_ref=source,
             dst_ref=target,
-            send_sem=relay_send.at[stage, side],
-            recv_sem=relay_recv.at[stage, side],
+            send_sem=relay_send.at[side],
+            recv_sem=relay_recv.at[side],
             device_id={"band": peer},
             device_id_type=pl.DeviceIdType.MESH,
         )
 
-    relays = [
-        (upper * half_rows, half_rows),
-        (second * level_rows, level_rows),
-        (third * level_rows, level_rows),
-    ]
-
-    def pass_on(stage):
-        @pl.when(me > 0)
-        def _():
-            relay(stage, me - 1, 0, *relays[stage]).start()
-
-        @pl.when(me < n - 1)
-        def _():
-            relay(stage, me + 1, 1, *relays[stage]).start()
+    to_left = jnp.logical_and(me > 0, me != n // 2)
+    to_right = jnp.logical_and(me < n - 1, me != n // 2 - 1)
+    middle = jnp.logical_or(me == n // 2, me == n // 2 - 1)
+
+    def pass_on():
+        @pl.when(to_left)
+        def _():
+            relay(me - 1, 0).start()
+
+        @pl.when(to_right)
+        def _():
+            relay(me + 1, 1).start()
 
     def take_ends():
-        for stage, (_, extent) in enumerate(relays):
-            region = block(extent, LANES)
-
-            @pl.when(me < n - 1)
-            def _():
-                pltpu.make_async_copy(region, region, relay_recv.at[stage, 0]).wait()
-
-            @pl.when(me > 0)
-            def _():
-                pltpu.make_async_copy(region, region, relay_recv.at[stage, 1]).wait()
+        @pl.when(to_right)
+        def _():
+            relay(me + 1, 0).wait_recv()
+
+        @pl.when(to_left)
+        def _():
+            relay(me - 1, 1).wait_recv()
+
+        @pl.when(middle)
+        def _():
+            settle(end_recv, height - rows, LANES)
+            settle(end_load, rows, LANES)
 
     def finish_relays():
-        for stage, (_, extent) in enumerate(relays):
-            region = block(extent, LANES)
-
-            @pl.when(me > 0)
-            def _():
-                pltpu.make_async_copy(region, region, relay_send.at[stage, 0]).wait()
-
-            @pl.when(me < n - 1)
-            def _():
-                pltpu.make_async_copy(region, region, relay_send.at[stage, 1]).wait()
-
-    def row_kernels(extent):
-        return jnp.concatenate(
-            [row_mats[k * UNIT : k * UNIT + extent, : extent + 2 * KH] for k in range(NK)], axis=0
-        )
-
-    def smear(start, extent, at, lo, span):
-        window = recv[
-            pl.ds(pl.multiple_of(start, KH), extent + 2 * KH), lo * LANES : (lo + span) * LANES
-        ]
-        smooth[at : at + NK * extent, lo * LANES : (lo + span) * LANES] = jnp.dot(
-            row_kernels(extent), window, preferred_element_type=F32
-        ).astype(BF16)
-
-    def render(start, extent, at, panels):
-        into = pl.multiple_of(EDGE + start, KH)
-        total = jnp.zeros((len(panels) * extent, LANES), F32)
-        for k in range(NK):
-            pieces = []
+        @pl.when(to_left)
+        def _():
+            relay(me - 1, 0).wait_send()
+
+        @pl.when(to_right)
+        def _():
+            relay(me + 1, 1).wait_send()
+
+        @pl.when(me != n // 2)
+        def _():
+            settle(end_send.at[1], rows, LANES)
+
+        @pl.when(me != n // 2 - 1)
+        def _():
+            settle(end_send.at[0], rows, LANES)
+
+    def across_kernels(panels, mats):
+        if mats is outer_mats:
+            windows = [ends[...]]
+        else:
+            windows = []
             for p in panels:
-                own = pl.ds(at + k * extent, extent)
                 if p == 0:
-                    piece = smooth[own, :LANES]
-                    pieces.append(jnp.concatenate([piece, piece], axis=1))
+                    piece = recv[:, :LANES]
+                    windows.append(jnp.concatenate([piece, piece], axis=1))
                 else:
-                    pieces.append(smooth[own, (p - 1) * LANES : (p + 1) * LANES])
-            field = jnp.dot(
-                jnp.concatenate(pieces, axis=0), column_mats[k], preferred_element_type=F32
-            )
-            total = total + weight_ref[k] * field * field
-        for i, p in enumerate(panels):
-            intensity[pl.ds(into, extent), p * LANES : (p + 1) * LANES] = total[
-                i * extent : (i + 1) * extent
-            ].astype(BF16)
-
-    def render_outer():
-        lane = lax.broadcasted_iota(jnp.int32, (height + 2 * KH, LANES), 1) < HALF
+                    windows.append(recv[:, (p - 1) * LANES : (p + 1) * LANES])
+        stacked = jnp.concatenate(windows, axis=0) if len(windows) > 1 else windows[0]
+        for pair in range(NK // 2):
+            result = jnp.dot(stacked, mats[pair], preferred_element_type=F32).astype(BF16)
+            for i, p in enumerate(panels):
+                for j in range(2):
+                    crossed[2 * pair + j, :, p * LANES : (p + 1) * LANES] = result[
+                        i * tall : (i + 1) * tall, j * LANES : (j + 1) * LANES
+                    ]
+
+    def gather_ends():
+        lane = lax.broadcasted_iota(jnp.int32, (tall, LANES), 1) < HALF
         ends[:, :LANES] = jnp.where(lane, after[...], before[...])
         ends[:, LANES:] = jnp.where(lane, recv[:, :LANES], recv[:, strip - LANES :])
-        start = 0
-        for extent in split(height):
-            lanes = lax.broadcasted_iota(jnp.int32, (extent, LANES), 1)
-            spread = jnp.dot(
-                row_kernels(extent), ends[start : start + extent + 2 * KH, :],
-                preferred_element_type=F32,
-            ).astype(BF16)
-            total = jnp.zeros((extent, LANES), F32)
-            for k in range(NK):
-                field = jnp.dot(
-                    spread[k * extent : (k + 1) * extent], outer_mats[k],
-                    preferred_element_type=F32,
-                )
-                total = total + weight_ref[k] * field * field
-            left = lanes < HALF
-            column = jnp.where(left, me * strip + lanes, me * strip + strip + lanes - HALF) - P_SIZE
-            total = jnp.where(jnp.logical_and(column >= 0, column < width), total, 0.0).astype(BF16)
-            into = slice(EDGE + start, EDGE + start + extent)
-            intensity[into, strip:] = total
-            intensity[into, :LANES] = jnp.where(lanes < LEAD, total, intensity[into, :LANES])
-            start += extent
+
+    def render(panels):
+        for g in range(0, len(panels), 2):
+            group = panels[g : g + 2]
+            start = 0
+            for extent in split(height):
+                total = jnp.zeros((extent, len(group) * LANES), F32)
+                for k in range(NK):
+                    window = slice(start, start + extent + 2 * KH)
+                    pieces = [crossed[k, window, p * LANES : (p + 1) * LANES] for p in group]
+                    field = jnp.dot(
+                        row_mats[k, :extent, : extent + 2 * KH],
+                        jnp.concatenate(pieces, axis=1) if len(pieces) > 1 else pieces[0],
+                        preferred_element_type=F32,
+                    )
+                    total = total + weight_ref[k] * field * field
+                into = slice(EDGE + start, EDGE + start + extent)
+                for i, p in enumerate(group):
+                    part = total[:, i * LANES : (i + 1) * LANES]
+                    if p == tiles:
+                        lanes = lax.broadcasted_iota(jnp.int32, (extent, LANES), 1)
+                        column = me * strip + lanes - P_SIZE + jnp.where(
+                            lanes < HALF, 0, strip - HALF
+                        )
+                        part = jnp.where(
+                            jnp.logical_and(column >= 0, column < width), part, 0.0
+                        ).astype(BF16)
+                        intensity[into, strip:] = part
+                        intensity[into, :LANES] = jnp.where(
+                            lanes < LEAD, part, intensity[into, :LANES]
+                        )
+                    else:
+                        intensity[into, p * LANES : (p + 1) * LANES] = part.astype(BF16)
+                start += extent
 
     def halfway(panels):
         runs = []
@@ -429,53 +442,38 @@
         partial_sums[:8, :] = first
         partial_sums[8:, :] = second
 
-    def whole(start, total):
-        at = 0
-        for extent in split(total):
-            smear(start + at, extent, 0, 0, tiles)
-            for p in range(0, tiles, 4):
-                render(start + at, extent, 0, list(range(p, min(p + 4, tiles))))
-            at += extent
-
     loads[-1].wait()
-    settle(recv_sem.at[0], *sizes[0])
-    pass_on(0)
-    whole(first_start, first_rows)
-    settle(recv_sem.at[1], *sizes[1])
-    pass_on(1)
-    whole(second_start, second_rows)
     loads[-2].wait()
-
-    seen, drawn, halves, done = set(), set(), set(), set()
+    seen, crossing, waiting, halves, done = set(), set(), [], set(), set()
     for e, event in enumerate(events):
-        settle(recv_sem.at[2 + e], *sizes[2 + e])
+        settle(recv_sem.at[e], *sizes[e])
         if e == 0:
-            pass_on(2)
+            pass_on()
+        send_after(e)
         for lo, span in event:
             seen.update(range(lo, lo + span))
         fresh = [
             p for p in range(tiles)
-            if p in seen and (p == 0 or p - 1 in seen) and p not in drawn
+            if p in seen and (p == 0 or p - 1 in seen) and p not in crossing
         ]
-        drawn.update(fresh)
-        at = 0
-        for extent in split(third_rows):
-            for lo, span in event:
-                smear(third_start + at, extent, NK * at, lo, span)
-            if fresh:
-                render(third_start + at, extent, NK * at, fresh)
-            at += extent
-        if e == max(len(events) - 2, 0):
+        if fresh:
+            across_kernels(fresh, column_mats)
+        crossing.update(fresh)
+        waiting += fresh
+        if e == min(1, len(events) - 1):
             take_ends()
-            render_outer()
-            drawn.add(tiles)
-        if tiles in drawn:
-            ready = drawn - halves
-            halfway(ready)
-            halves.update(ready)
-            targets = {q for q in range(tiles) if q in halves and q + 1 in halves} - done
-            finish(targets)
-            done.update(targets)
+            gather_ends()
+            across_kernels([tiles], outer_mats)
+            waiting.append(tiles)
+        if e == 0 and len(events) > 1:
+            continue
+        render(waiting)
+        halfway(waiting)
+        halves.update(waiting)
+        waiting = []
+        targets = {q for q in range(tiles) if q in halves and q + 1 in halves} - done
+        finish(targets)
+        done.update(targets)
 
     stats_mine[0:1, :] = jnp.sum(partial_sums[:8, :], axis=0, keepdims=True)
     stats_mine[1:2, :] = jnp.sum(partial_sums[8:, :], axis=0, keepdims=True)
@@ -484,52 +482,27 @@
         return pltpu.make_async_remote_copy(
             src_ref=stats_mine,
             dst_ref=stats_all.at[me],
-            send_sem=stat_send.at[peer],
-            recv_sem=stat_recv.at[me],
+            send_sem=stat_send,
+            recv_sem=stat_recv,
             device_id={"band": peer},
             device_id_type=pl.DeviceIdType.MESH,
         )
 
-    def stat_from(peer):
-        return pltpu.make_async_remote_copy(
-            src_ref=stats_mine,
-            dst_ref=stats_all.at[peer],
-            send_sem=stat_send.at[peer],
-            recv_sem=stat_recv.at[peer],
-            device_id={"band": peer},
-            device_id_type=pl.DeviceIdType.MESH,
-        )
-
-    def send_stats(i, carry):
-        peer = lax.rem(me + n // 2 + i, n)
-
-        @pl.when(peer != me)
-        def _():
-            stat_to(peer).start()
-
-        return carry
-
-    lax.fori_loop(0, n, send_stats, 0)
+    for i in range(n - 1, 0, -1):
+        stat_to(partner(i)).start()
     stats_all[me] = stats_mine[...]
 
     for slot, size in enumerate(sizes):
         settle(send_sem.at[slot], *size)
     finish_relays()
 
-    def take_stats(i, carry):
-        peer = lax.rem(me + i, n)
-        stat_from(peer).wait_recv()
-        stat_to(peer).wait_send()
-        return carry
-
-    lax.fori_loop(1, n, take_stats, 0)
-
-    sums = lax.fori_loop(
-        0, n, lambda i, carry: carry + stats_all[i], jnp.zeros((2, LANES), F32)
-    )
+    others = stats_all.at[pl.ds(0, n - 1)]
+    pltpu.make_async_copy(others, others, stat_send).wait()
+    pltpu.make_async_copy(others, others, stat_recv).wait()
+    sums = jnp.sum(stats_all[...], axis=0)
     cells = height * width
-    mean = jnp.sum(sums[0:1], axis=1, keepdims=True) / cells
-    power = jnp.sum(sums[1:2], axis=1, keepdims=True) / cells
+    totals = jnp.sum(sums, axis=1, keepdims=True) / cells
+    mean, power = totals[0:1], totals[1:2]
     scale = lax.rsqrt(power - mean * mean + epsilon)
     mean_ref[...] = jnp.broadcast_to(mean, (1, strip))
     for b in range(count):
@@ -544,7 +517,7 @@
     height, strip = image.shape
     wide = strip + LANES
     count = height // BLK
-    slots = 2 + len(plan(strip // LANES))
+    slots = len(plan(strip // LANES))
     tall = height + 2 * KH
     hbm = pl.BlockSpec(memory_space=pltpu.HBM)
     vmem = pl.BlockSpec(memory_space=pltpu.VMEM)
@@ -570,13 +543,13 @@
             pltpu.VMEM((tall, LANES), BF16),
             pltpu.VMEM((tall, 2 * LANES), BF16),
             pltpu.VMEM((height, strip), BF16),
-            pltpu.VMEM((NK * UNIT, 2 * LANES), BF16),
-            pltpu.VMEM((NK, 2 * LANES, LANES), BF16),
-            pltpu.VMEM((NK, 2 * LANES, LANES), BF16),
+            pltpu.VMEM((NK, UNIT, 2 * LANES), BF16),
+            pltpu.VMEM((NK // 2, 2 * LANES, 2 * LANES), BF16),
+            pltpu.VMEM((NK // 2, 2 * LANES, 2 * LANES), BF16),
             pltpu.VMEM((count, BLK, 2 * LANES), BF16),
             pltpu.VMEM((count, 2 * LANES, LANES), BF16),
             pltpu.VMEM((count, 2 * LANES, LANES), BF16),
-            pltpu.VMEM((NK * max(UNIT, height // LEVELS + 2 * KH), strip), BF16),
+            pltpu.VMEM((NK, tall, wide), BF16),
             pltpu.VMEM((height + 2 * EDGE, wide), BF16),
             pltpu.VMEM((height, wide), BF16),
             pltpu.VMEM((height + 16, strip), F32),
@@ -585,10 +558,13 @@
             pltpu.VMEM((n, 2, LANES), F32),
             pltpu.SemaphoreType.DMA((slots,)),
             pltpu.SemaphoreType.DMA((slots,)),
-            pltpu.SemaphoreType.DMA((3, 2)),
-            pltpu.SemaphoreType.DMA((3, 2)),
-            pltpu.SemaphoreType.DMA((n,)),
-            pltpu.SemaphoreType.DMA((n,)),
+            pltpu.SemaphoreType.DMA((2,)),
+            pltpu.SemaphoreType.DMA((2,)),
+            pltpu.SemaphoreType.DMA((2,)),
+            pltpu.SemaphoreType.DMA,
+            pltpu.SemaphoreType.DMA,
+            pltpu.SemaphoreType.DMA,
+            pltpu.SemaphoreType.DMA,
             pltpu.SemaphoreType.DMA((9,)),
         ],
         compiler_params=pltpu.CompilerParams(

time: 28.6 us -> 26.7 us (0.934)
  Pallas kernels: 27.6 us -> 25.6 us
    pallas_call x1, Pallas kernels: 27.6 us -> 25.6 us  [on_device(): pl.pallas_call(functools.partial(kernel, n, height, width), out_shape=(ja...]
where the time goes in v2:
time: 26.7 us; the launch traced here: 26.5 us
  Pallas kernels  25.6 us (96%)
  other arithmetic  0.92 us (3%)
    pallas_call x1, Pallas kernels, on_device(): pl.pallas_call(functools.partial(kernel, n, height, width), out_shape=(ja...  25.6 us
    convert_element_type x1, other arithmetic, on_device(): return out.reshape(height, strip).astype(BF16)  0.92 us

profile of v2, /device:TPU:0, one launch (start us, length us, event | category | flops | bytes accessed | tf_op | source)
XLA Modules:
  0.0 26.5 jit_solution(1652739765138451820)
XLA Ops:
  0.0 25.6 %shard_map.91 = (f32[256,1024]{1,0:T(8,128)S(1)}, f32[1,1024]{1,0:T(1,128)S(1)}, f32[2,1024]{1,0:T(2,128)S(1)}) custom-call(f32[8]{0:T(128)} %weight_hbm.1, s32[2,1,2]{2,1,0:T(1,128)} %bitcast.15, s32[2,1,2]{2,1,0:T(1,128)} %bitcast.16, s32[1,2]{1,0:T(1,128)} %bitcast.17, bf16[16,16384]{1,0:T(8,128)(2,1)} %design_hbm.1, bf16[8,33]{1,0:T(8,128)(2,1)} %row_hbm.1, ...), custom_call_target="tpu_custom_call" | custom-call | tf_op jit(solution)/shard_map/pallas_call | solution.py:524
  25.6 0.9 %fusion = bf16[256,1024]{1,0:T(8,128)(2,1)} fusion(f32[256,1024]{1,0:T(8,128)S(1)} %get-tuple-element.8, f32[2,1024]{1,0:T(2,128)S(1)} %get-tuple-element.10, f32[1024]{0:T(1024)S(1)} %bitcast.13), kind=kLoop, calls=%fused_computation.1 | loop fusion | flops 786432 | bytes 1585152 | tf_op jit(solution)/shard_map/convert_element_type | solution.py:586

commit v3 on v2

--- a/solution.py
+++ b/solution.py
@@ -21,8 +21,7 @@
 INNER = LANES - LEAD
 
 LEVELS = 4
-INNER_SENDS = {3: 0}
-OUTER_SENDS = {3: 0}
+LATE = (3,)
 
 epsilon = 1e-05
 
@@ -67,7 +66,7 @@
     recv, before, after, ends, image, row_mats, column_mats, outer_mats,
     warp_rows, warp_columns, warp_last, crossed, intensity, partial,
     diff, partial_sums, stats_mine, stats_all,
-    send_sem, recv_sem, relay_send, relay_recv, end_send, end_recv, end_load, stat_send, stat_recv, load_sem,
+    send_sem, recv_sem, relay_send, relay_recv, end_send, end_recv, end_load, stat_send, stat_recv, two_away, three_away, load_sem,
 ):
     me = lax.axis_index("band")
     rows = height // n
@@ -78,15 +77,6 @@
     events = plan(tiles)
 
     barrier = pltpu.get_barrier_semaphore()
-
-    def greet(i, carry):
-        peer = lax.rem(me + i, n)
-        pl.semaphore_signal(
-            barrier, inc=1, device_id={"band": peer}, device_id_type=pl.DeviceIdType.MESH
-        )
-        return carry
-
-    lax.fori_loop(1, n, greet, 0)
 
     mine = pl.ds(pl.multiple_of(KH + me * rows, rows), rows)
     loads = [
@@ -108,9 +98,6 @@
             ]
         )
     ]
-    for load in loads:
-        load.start()
-
     flips = {}
     bit = 1
     while bit < n:
@@ -160,34 +147,82 @@
 
     sizes = [(height - rows, sum(span for _, span in event) * LANES) for event in events]
 
-    pl.semaphore_wait(barrier, n - 1)
-
-    def send_pieces(chosen_events):
-        for e in chosen_events:
-            for i in range(1, n):
-                for lo, span in events[e]:
-                    send(partner(i), e, lo, span)
-
-    def send_after(e):
-        for mine_too, schedule in ((True, INNER_SENDS), (False, OUTER_SENDS)):
-            batch = [x for x in range(1, len(events)) if schedule.get(x, -1) == e]
-            if batch:
-                @pl.when(inner == mine_too)
-                def _():
-                    send_pieces(batch)
-
     level = me // (n // LEVELS)
     inner = jnp.logical_and(level > 0, level < LEVELS - 1)
-    send_pieces([0])
+    outer = jnp.logical_not(inner)
+    near = range(1, n // 2)
+    second = range(n // 2, 3 * n // 4)
+    third = range(3 * n // 4, n)
+
+    def send_to(e, ids):
+        for i in ids:
+            for lo, span in events[e]:
+                send(partner(i), e, lo, span)
+
+    def tell(semaphore, i):
+        pl.semaphore_signal(
+            semaphore, inc=1, device_id={"band": partner(i)}, device_id_type=pl.DeviceIdType.MESH
+        )
+
+    for i in near:
+        tell(barrier, i)
+
+    @pl.when(inner)
+    def _():
+        for i in third:
+            tell(barrier, i)
+
+    for load in loads:
+        load.start()
+    pl.semaphore_wait(barrier, n // 2 - 1 + jnp.where(inner, n // 4, 0))
+    early = range(1, min(2, len(events)))
+
+    @pl.when(inner)
+    def _():
+        tell(two_away, n // LEVELS)
+        tell(two_away, 3 * n // LEVELS)
+
+    send_to(0, near)
+
+    @pl.when(inner)
+    def _():
+        send_to(0, third)
+
+        @pl.when(level == 1)
+        def _():
+            for e in early:
+                send_to(e, third)
+
+        pl.semaphore_wait(two_away, 1)
+        tell(three_away, n // LEVELS)
+        send_to(0, second)
+
+    @pl.when(outer)
+    def _():
+        pl.semaphore_wait(two_away, 1)
+        send_to(0, second)
+        pl.semaphore_wait(three_away, 1)
+        send_to(0, third)
+
     send_ends()
-    send_after(-1)
-
-    zero_rows = jnp.zeros((KH, LANES), BF16)
-    for edge in (before, after):
-        edge[:KH, :] = zero_rows
-        edge[KH + height :, :] = zero_rows
-    recv[:KH, :] = jnp.zeros((KH, strip), BF16)
-    recv[KH + height :, :] = jnp.zeros((KH, strip), BF16)
+    for e in early:
+        send_to(e, near)
+        send_to(e, second)
+
+        @pl.when(jnp.logical_not(level == 1))
+        def _():
+            send_to(e, third)
+
+    def send_rest(late):
+        for e in range(2, len(events)):
+            if (e in LATE) == late:
+                send_to(e, range(1, n))
+
+    send_rest(False)
+
+    for k in range(NK):
+        crossed[k, :KH, :] = jnp.zeros((KH, strip + LANES), BF16)
+        crossed[k, KH + height :, :] = jnp.zeros((KH, strip + LANES), BF16)
 
     @pl.when(me == 0)
     def _():
@@ -321,6 +356,8 @@
         def _():
             settle(end_send.at[0], rows, LANES)
 
+    body = slice(KH, KH + height)
+
     def across_kernels(panels, mats):
         if mats is outer_mats:
             windows = [ends[...]]
@@ -328,23 +365,23 @@
             windows = []
             for p in panels:
                 if p == 0:
-                    piece = recv[:, :LANES]
+                    piece = recv[body, :LANES]
                     windows.append(jnp.concatenate([piece, piece], axis=1))
                 else:
-                    windows.append(recv[:, (p - 1) * LANES : (p + 1) * LANES])
+                    windows.append(recv[body, (p - 1) * LANES : (p + 1) * LANES])
         stacked = jnp.concatenate(windows, axis=0) if len(windows) > 1 else windows[0]
         for pair in range(NK // 2):
             result = jnp.dot(stacked, mats[pair], preferred_element_type=F32).astype(BF16)
             for i, p in enumerate(panels):
                 for j in range(2):
-                    crossed[2 * pair + j, :, p * LANES : (p + 1) * LANES] = result[
-                        i * tall : (i + 1) * tall, j * LANES : (j + 1) * LANES
+                    crossed[2 * pair + j, body, p * LANES : (p + 1) * LANES] = result[
+                        i * height : (i + 1) * height, j * LANES : (j + 1) * LANES
                     ]
 
     def gather_ends():
-        lane = lax.broadcasted_iota(jnp.int32, (tall, LANES), 1) < HALF
-        ends[:, :LANES] = jnp.where(lane, after[...], before[...])
-        ends[:, LANES:] = jnp.where(lane, recv[:, :LANES], recv[:, strip - LANES :])
+        lane = lax.broadcasted_iota(jnp.int32, (height, LANES), 1) < HALF
+        ends[:, :LANES] = jnp.where(lane, after[body, :], before[body, :])
+        ends[:, LANES:] = jnp.where(lane, recv[body, :LANES], recv[body, strip - LANES :])
 
     def render(panels):
         for g in range(0, len(panels), 2):
@@ -445,11 +482,13 @@
     loads[-1].wait()
     loads[-2].wait()
     seen, crossing, waiting, halves, done = set(), set(), [], set(), set()
+    halves_due = []
     for e, event in enumerate(events):
         settle(recv_sem.at[e], *sizes[e])
         if e == 0:
             pass_on()
-        send_after(e)
+        if e == 0:
+            send_rest(True)
         for lo, span in event:
             seen.update(range(lo, lo + span))
         fresh = [
@@ -465,9 +504,13 @@
             gather_ends()
             across_kernels([tiles], outer_mats)
             waiting.append(tiles)
+        render(waiting)
         if e == 0 and len(events) > 1:
+            halves_due = waiting
+            waiting = []
             continue
-        render(waiting)
+        waiting = halves_due + waiting
+        halves_due = []
         halfway(waiting)
         halves.update(waiting)
         waiting = []
@@ -541,7 +584,7 @@
             pltpu.VMEM((tall, strip), BF16),
             pltpu.VMEM((tall, LANES), BF16),
             pltpu.VMEM((tall, LANES), BF16),
-            pltpu.VMEM((tall, 2 * LANES), BF16),
+            pltpu.VMEM((height, 2 * LANES), BF16),
             pltpu.VMEM((height, strip), BF16),
             pltpu.VMEM((NK, UNIT, 2 * LANES), BF16),
             pltpu.VMEM((NK // 2, 2 * LANES, 2 * LANES), BF16),
@@ -565,6 +608,8 @@
             pltpu.SemaphoreType.DMA,
             pltpu.SemaphoreType.DMA,
             pltpu.SemaphoreType.DMA,
+            pltpu.SemaphoreType.REGULAR,
+            pltpu.SemaphoreType.REGULAR,
             pltpu.SemaphoreType.DMA((9,)),
         ],
         compiler_params=pltpu.CompilerParams(

time: 26.7 us -> 25.5 us (0.955)
  Pallas kernels: 25.6 us -> 24.4 us
    pallas_call x1, Pallas kernels: 25.6 us -> 24.4 us  [on_device(): pl.pallas_call(functools.partial(kernel, n, height, width), out_shape=(ja...]
where the time goes in v3:
time: 25.5 us; the launch traced here: 25.4 us
  Pallas kernels  24.4 us (96%)
  other arithmetic  0.92 us (4%)
    pallas_call x1, Pallas kernels, on_device(): pl.pallas_call(functools.partial(kernel, n, height, width), out_shape=(ja...  24.4 us
    convert_element_type x1, other arithmetic, on_device(): return out.reshape(height, strip).astype(BF16)  0.92 us

profile of v3, /device:TPU:0, one launch (start us, length us, event | category | flops | bytes accessed | tf_op | source)
XLA Modules:
  0.0 25.4 jit_solution(18388890522852740956)
XLA Ops:
  0.0 24.4 %shard_map.91 = (f32[256,1024]{1,0:T(8,128)S(1)}, f32[1,1024]{1,0:T(1,128)S(1)}, f32[2,1024]{1,0:T(2,128)S(1)}) custom-call(f32[8]{0:T(128)} %weight_hbm.1, s32[2,1,2]{2,1,0:T(1,128)} %bitcast.15, s32[2,1,2]{2,1,0:T(1,128)} %bitcast.16, s32[1,2]{1,0:T(1,128)} %bitcast.17, bf16[16,16384]{1,0:T(8,128)(2,1)} %design_hbm.1, bf16[8,33]{1,0:T(8,128)(2,1)} %row_hbm.1, ...), custom_call_target="tpu_custom_call" | custom-call | tf_op jit(solution)/shard_map/pallas_call | solution.py:567
  24.4 0.9 %fusion = bf16[256,1024]{1,0:T(8,128)(2,1)} fusion(f32[256,1024]{1,0:T(8,128)S(1)} %get-tuple-element.8, f32[2,1024]{1,0:T(2,128)S(1)} %get-tuple-element.10, f32[1024]{0:T(1024)S(1)} %bitcast.13), kind=kLoop, calls=%fused_computation.1 | loop fusion | flops 786432 | bytes 1585152 | tf_op jit(solution)/shard_map/convert_element_type | solution.py:631

commit v4 on v3

--- a/solution.py
+++ b/solution.py
@@ -15,6 +15,7 @@
 LANES = 128
 HALF = LANES // 2
 EDGE = 32
+PIECE = 64
 UNIT = 128
 REACH = 2 * KH + 1
 LEAD = P_SIZE + KH
@@ -107,14 +108,14 @@
     def partner(i):
         return me + sum(flip for bit, flip in flips.items() if i & bit)
 
-    def send(peer, slot, lo, span):
+    def send(peer, slot, lo, span, far):
         pltpu.make_async_remote_copy(
             src_ref=design_hbm.at[
                 :, pl.ds(pl.multiple_of(peer * strip + lo * LANES, LANES), span * LANES)
             ],
             dst_ref=recv.at[mine, pl.ds(lo * LANES, span * LANES)],
-            send_sem=send_sem.at[slot],
-            recv_sem=recv_sem.at[slot],
+            send_sem=send_sem.at[slot, far],
+            recv_sem=recv_sem.at[slot, far],
             device_id={"band": peer},
             device_id_type=pl.DeviceIdType.MESH,
         ).start()
@@ -145,7 +146,8 @@
     def settle(sem, extent, columns):
         pltpu.make_async_copy(block(extent, columns), block(extent, columns), sem).wait()
 
-    sizes = [(height - rows, sum(span for _, span in event) * LANES) for event in events]
+    half_rows = height // 2
+    sizes = [sum(span for _, span in event) * LANES for event in events]
 
     level = me // (n // LEVELS)
     inner = jnp.logical_and(level > 0, level < LEVELS - 1)
@@ -157,7 +159,7 @@
     def send_to(e, ids):
         for i in ids:
             for lo, span in events[e]:
-                send(partner(i), e, lo, span)
+                send(partner(i), e, lo, span, int(i >= n // 2))
 
     def tell(semaphore, i):
         pl.semaphore_signal(
@@ -214,9 +216,24 @@
             send_to(e, third)
 
     def send_rest(late):
+        if not late:
+            for e in range(2, len(events)):
+                send_to(e, near)
         for e in range(2, len(events)):
             if (e in LATE) == late:
-                send_to(e, range(1, n))
+                if not late:
+                    send_to(e, range(n // 2, n))
+                    continue
+
+                @pl.when(inner)
+                def _():
+                    send_to(e, second)
+                    send_to(e, third)
+
+                @pl.when(outer)
+                def _():
+                    send_to(e, third)
+                    send_to(e, second)
 
     send_rest(False)
 
@@ -357,8 +374,12 @@
             settle(end_send.at[0], rows, LANES)
 
     body = slice(KH, KH + height)
-
-    def across_kernels(panels, mats):
+    upper = level // (LEVELS // 2)
+    near_start = upper * half_rows
+    far_start = half_rows - near_start
+
+    def across_kernels(panels, mats, start, extent):
+        body = pl.ds(pl.multiple_of(KH + start, KH), extent)
         if mats is outer_mats:
             windows = [ends[...]]
         else:
@@ -375,7 +396,7 @@
             for i, p in enumerate(panels):
                 for j in range(2):
                     crossed[2 * pair + j, body, p * LANES : (p + 1) * LANES] = result[
-                        i * height : (i + 1) * height, j * LANES : (j + 1) * LANES
+                        i * extent : (i + 1) * extent, j * LANES : (j + 1) * LANES
                     ]
 
     def gather_ends():
@@ -481,33 +502,51 @@
 
     loads[-1].wait()
     loads[-2].wait()
-    seen, crossing, waiting, halves, done = set(), set(), [], set(), set()
-    halves_due = []
-    for e, event in enumerate(events):
-        settle(recv_sem.at[e], *sizes[e])
-        if e == 0:
-            pass_on()
-        if e == 0:
-            send_rest(True)
+    fresh_of, seen, crossing = [], set(), set()
+    for event in events:
         for lo, span in event:
             seen.update(range(lo, lo + span))
         fresh = [
             p for p in range(tiles)
             if p in seen and (p == 0 or p - 1 in seen) and p not in crossing
         ]
-        if fresh:
-            across_kernels(fresh, column_mats)
         crossing.update(fresh)
-        waiting += fresh
+        fresh_of.append(fresh)
+
+    def begin(e):
+        settle_near(e)
+        if fresh_of[e]:
+            across_kernels(fresh_of[e], column_mats, near_start, half_rows)
+
+    def settle_near(e):
+        settle(recv_sem.at[e, 0], half_rows - rows, sizes[e])
+
+    def settle_far(e):
+        settle(recv_sem.at[e, 1], half_rows, sizes[e])
+
+    settle_near(0)
+    halves_due = []
+    waiting, halves, done = [], set(), set()
+    for e, event in enumerate(events):
+        settle_far(e)
+        if e == 0:
+            pass_on()
+            send_rest(True)
+            if fresh_of[0]:
+                across_kernels(fresh_of[0], column_mats, 0, height)
+        elif fresh_of[e]:
+            across_kernels(fresh_of[e], column_mats, far_start, half_rows)
+        waiting += fresh_of[e]
         if e == min(1, len(events) - 1):
             take_ends()
             gather_ends()
-            across_kernels([tiles], outer_mats)
+            across_kernels([tiles], outer_mats, 0, height)
             waiting.append(tiles)
         render(waiting)
         if e == 0 and len(events) > 1:
             halves_due = waiting
             waiting = []
+            begin(1)
             continue
         waiting = halves_due + waiting
         halves_due = []
@@ -517,6 +556,9 @@
         targets = {q for q in range(tiles) if q in halves and q + 1 in halves} - done
         finish(targets)
         done.update(targets)
+        if e == 1:
+            for later in range(2, len(events)):
+                begin(later)
 
     stats_mine[0:1, :] = jnp.sum(partial_sums[:8, :], axis=0, keepdims=True)
     stats_mine[1:2, :] = jnp.sum(partial_sums[8:, :], axis=0, keepdims=True)
@@ -531,12 +573,17 @@
             device_id_type=pl.DeviceIdType.MESH,
         )
 
-    for i in range(n - 1, 0, -1):
-        stat_to(partner(i)).start()
+    for peer in range(n):
+
+        @pl.when(me != peer)
+        def _():
+            stat_to(jnp.int32(peer)).start()
+
     stats_all[me] = stats_mine[...]
 
-    for slot, size in enumerate(sizes):
-        settle(send_sem.at[slot], *size)
+    for e, columns in enumerate(sizes):
+        settle(send_sem.at[e, 0], half_rows - rows, columns)
+        settle(send_sem.at[e, 1], half_rows, columns)
     finish_relays()
 
     others = stats_all.at[pl.ds(0, n - 1)]
@@ -550,6 +597,22 @@
     mean_ref[...] = jnp.broadcast_to(mean, (1, strip))
     for b in range(count):
         scale_ref[b : b + 1, :] = jnp.broadcast_to(care_ref[0, b].astype(F32) * scale, (1, strip))
+
+
+def normalize(filtered, mean, scale, out, held, sem):
+    height = filtered.shape[0]
+    copies = []
+    for at in range(0, height, PIECE):
+        rows = slice(at, at + PIECE)
+        b = at // BLK
+        held[rows, :] = ((filtered[rows, :] - mean[...]) * scale[b : b + 1, :]).astype(BF16)
+        copy = pltpu.make_async_copy(
+            held.at[pl.ds(at, PIECE), :], out.at[pl.ds(at, PIECE), :], sem.at[at // PIECE]
+        )
+        copy.start()
+        copies.append(copy)
+    for copy in copies:
+        copy.wait()
 
 
 def on_device(
@@ -599,8 +662,8 @@
             pltpu.VMEM((16, LANES), F32),
             pltpu.VMEM((2, LANES), F32),
             pltpu.VMEM((n, 2, LANES), F32),
-            pltpu.SemaphoreType.DMA((slots,)),
-            pltpu.SemaphoreType.DMA((slots,)),
+            pltpu.SemaphoreType.DMA((slots, 2)),
+            pltpu.SemaphoreType.DMA((slots, 2)),
             pltpu.SemaphoreType.DMA((2,)),
             pltpu.SemaphoreType.DMA((2,)),
             pltpu.SemaphoreType.DMA((2,)),
@@ -626,9 +689,17 @@
         pin(interp.T),
         pin(image),
     )
-    blocks = filtered.reshape(count, BLK, strip)
-    out = (blocks - mean[:, None]) * scale[:, None]
-    return out.reshape(height, strip).astype(BF16)
+    return pl.pallas_call(
+        normalize,
+        out_shape=jax.ShapeDtypeStruct((height, strip), BF16),
+        in_specs=[vmem] * 3,
+        out_specs=hbm,
+        scratch_shapes=[
+            pltpu.VMEM((height, strip), BF16),
+            pltpu.SemaphoreType.DMA((height // PIECE,)),
+        ],
+        compiler_params=pltpu.CompilerParams(vmem_limit_bytes=8 * 1024 * 1024),
+    )(filtered, mean, scale)
 
 
 def solution(mesh):

time: 25.5 us -> 25.4 us (level)
  other arithmetic: 0.92 us -> 0 us
  Pallas kernels: 24.4 us -> 25.2 us
    convert_element_type x1 -> x0, other arithmetic: 0.92 us -> none  [on_device(): return out.reshape(height, strip).astype(BF16)]
    pallas_call x0 -> x1, Pallas kernels: none -> 0.85 us  [on_device(): pl.pallas_call(normalize, out_shape=jax.ShapeDtypeStruct((height, strip),...]
where the time goes in v4:
time: 25.4 us; the launch traced here: 25.2 us
  Pallas kernels  25.2 us (99%)
    pallas_call x1, Pallas kernels, on_device(): pl.pallas_call(functools.partial(kernel, n, height, width), out_shape=(ja...  24.4 us
    pallas_call x1, Pallas kernels, on_device(): pl.pallas_call(normalize, out_shape=jax.ShapeDtypeStruct((height, strip),...  0.85 us

profile of v4, /device:TPU:0, one launch (start us, length us, event | category | flops | bytes accessed | tf_op | source)
XLA Modules:
  0.0 25.2 jit_solution(7320032230858982276)
XLA Ops:
  0.0 24.4 %shard_map.91 = (f32[256,1024]{1,0:T(8,128)S(1)}, f32[1,1024]{1,0:T(1,128)S(1)}, f32[2,1024]{1,0:T(2,128)S(1)}) custom-call(f32[8]{0:T(128)} %weight_hbm.1, s32[2,1,2]{2,1,0:T(1,128)} %bitcast.9, s32[2,1,2]{2,1,0:T(1,128)} %bitcast.10, s32[1,2]{1,0:T(1,128)} %bitcast.11, bf16[16,16384]{1,0:T(8,128)(2,1)} %design_hbm.1, bf16[8,33]{1,0:T(8,128)(2,1)} %row_hbm.1, ...), custom_call_target="tpu_custom_call" | custom-call | tf_op jit(solution)/shard_map/pallas_call | solution.py:630
  24.4 0.8 %shard_map.92 = bf16[256,1024]{1,0:T(8,128)(2,1)} custom-call(f32[256,1024]{1,0:T(8,128)S(1)} %get-tuple-element.8.filtered, f32[1,1024]{1,0:T(1,128)S(1)} %get-tuple-element.9.mean, f32[2,1024]{1,0:T(2,128)S(1)} %get-tuple-element.10.scale), custom_call_target="tpu_custom_call" | custom-call | tf_op jit(solution)/shard_map/pallas_call | solution.py:692

commit v5 on v4

--- a/solution.py
+++ b/solution.py
@@ -16,7 +16,7 @@
 HALF = LANES // 2
 EDGE = 32
 PIECE = 64
-UNIT = 128
+UNIT = 144
 REACH = 2 * KH + 1
 LEAD = P_SIZE + KH
 INNER = LANES - LEAD
@@ -404,14 +404,20 @@
         ends[:, :LANES] = jnp.where(lane, after[body, :], before[body, :])
         ends[:, LANES:] = jnp.where(lane, recv[body, :LANES], recv[body, strip - LANES :])
 
-    def render(panels):
+    def rows_at(start, extent):
+        if isinstance(start, int):
+            return slice(start, start + extent)
+        return pl.ds(pl.multiple_of(start, KH), extent)
+
+    def render(panels, first, total_rows):
         for g in range(0, len(panels), 2):
             group = panels[g : g + 2]
-            start = 0
-            for extent in split(height):
+            at = 0
+            for extent in split(total_rows):
+                start = first + at
                 total = jnp.zeros((extent, len(group) * LANES), F32)
+                window = rows_at(start, extent + 2 * KH)
                 for k in range(NK):
-                    window = slice(start, start + extent + 2 * KH)
                     pieces = [crossed[k, window, p * LANES : (p + 1) * LANES] for p in group]
                     field = jnp.dot(
                         row_mats[k, :extent, : extent + 2 * KH],
@@ -419,7 +425,7 @@
                         preferred_element_type=F32,
                     )
                     total = total + weight_ref[k] * field * field
-                into = slice(EDGE + start, EDGE + start + extent)
+                into = rows_at(EDGE + start, extent)
                 for i, p in enumerate(group):
                     part = total[:, i * LANES : (i + 1) * LANES]
                     if p == tiles:
@@ -436,7 +442,7 @@
                         )
                     else:
                         intensity[into, p * LANES : (p + 1) * LANES] = part.astype(BF16)
-                start += extent
+                at += extent
 
     def halfway(panels):
         runs = []
@@ -517,6 +523,7 @@
         settle_near(e)
         if fresh_of[e]:
             across_kernels(fresh_of[e], column_mats, near_start, half_rows)
+            render(fresh_of[e], upper * (half_rows + KH), half_rows - KH)
 
     def settle_near(e):
         settle(recv_sem.at[e, 0], half_rows - rows, sizes[e])
@@ -534,19 +541,22 @@
             send_rest(True)
             if fresh_of[0]:
                 across_kernels(fresh_of[0], column_mats, 0, height)
+                render(fresh_of[0], 0, height)
         elif fresh_of[e]:
             across_kernels(fresh_of[e], column_mats, far_start, half_rows)
+            render(fresh_of[e], (1 - upper) * (half_rows - KH), half_rows + KH)
         waiting += fresh_of[e]
         if e == min(1, len(events) - 1):
             take_ends()
             gather_ends()
             across_kernels([tiles], outer_mats, 0, height)
+            render([tiles], 0, height)
             waiting.append(tiles)
-        render(waiting)
         if e == 0 and len(events) > 1:
             halves_due = waiting
             waiting = []
-            begin(1)
+            for later in range(1, len(events)):
+                begin(later)
             continue
         waiting = halves_due + waiting
         halves_due = []
@@ -556,9 +566,6 @@
         targets = {q for q in range(tiles) if q in halves and q + 1 in halves} - done
         finish(targets)
         done.update(targets)
-        if e == 1:
-            for later in range(2, len(events)):
-                begin(later)
 
     stats_mine[0:1, :] = jnp.sum(partial_sums[:8, :], axis=0, keepdims=True)
     stats_mine[1:2, :] = jnp.sum(partial_sums[8:, :], axis=0, keepdims=True)

time: 25.4 us -> 25.3 us (level)
  no operation moved by 1% of the time
where the time goes in v5:
time: 25.3 us; the launch traced here: 25.1 us
  Pallas kernels  25.1 us (99%)
    pallas_call x1, Pallas kernels, on_device(): pl.pallas_call(functools.partial(kernel, n, height, width), out_shape=(ja...  24.3 us
    pallas_call x1, Pallas kernels, on_device(): pl.pallas_call(normalize, out_shape=jax.ShapeDtypeStruct((height, strip),...  0.85 us

profile of v5, /device:TPU:0, one launch (start us, length us, event | category | flops | bytes accessed | tf_op | source)
XLA Modules:
  0.0 25.1 jit_solution(11007287480554088164)
XLA Ops:
  0.0 24.3 %shard_map.91 = (f32[256,1024]{1,0:T(8,128)S(1)}, f32[1,1024]{1,0:T(1,128)S(1)}, f32[2,1024]{1,0:T(2,128)S(1)}) custom-call(f32[8]{0:T(128)} %weight_hbm.1, s32[2,1,2]{2,1,0:T(1,128)} %bitcast.9, s32[2,1,2]{2,1,0:T(1,128)} %bitcast.10, s32[1,2]{1,0:T(1,128)} %bitcast.11, bf16[16,16384]{1,0:T(8,128)(2,1)} %design_hbm.1, bf16[8,33]{1,0:T(8,128)(2,1)} %row_hbm.1, ...), custom_call_target="tpu_custom_call" | custom-call | tf_op jit(solution)/shard_map/pallas_call | solution.py:637
  24.3 0.8 %shard_map.92 = bf16[256,1024]{1,0:T(8,128)(2,1)} custom-call(f32[256,1024]{1,0:T(8,128)S(1)} %get-tuple-element.8.filtered, f32[1,1024]{1,0:T(1,128)S(1)} %get-tuple-element.9.mean, f32[2,1024]{1,0:T(2,128)S(1)} %get-tuple-element.10.scale), custom_call_target="tpu_custom_call" | custom-call | tf_op jit(solution)/shard_map/pallas_call | solution.py:699

commit v6 on v5

--- a/solution.py
+++ b/solution.py
@@ -22,7 +22,7 @@
 INNER = LANES - LEAD
 
 LEVELS = 4
-LATE = (3,)
+LATE = ()
 
 epsilon = 1e-05
 

time: 25.3 us -> 25.3 us (level)
  no operation moved by 1% of the time
where the time goes in v6:
time: 25.3 us; the launch traced here: 25.1 us
  Pallas kernels  25.1 us (99%)
    pallas_call x1, Pallas kernels, on_device(): pl.pallas_call(functools.partial(kernel, n, height, width), out_shape=(ja...  24.3 us
    pallas_call x1, Pallas kernels, on_device(): pl.pallas_call(normalize, out_shape=jax.ShapeDtypeStruct((height, strip),...  0.85 us

profile of v6, /device:TPU:0, one launch (start us, length us, event | category | flops | bytes accessed | tf_op | source)
XLA Modules:
  0.0 25.1 jit_solution(11676802049085387921)
XLA Ops:
  0.0 24.3 %shard_map.91 = (f32[256,1024]{1,0:T(8,128)S(1)}, f32[1,1024]{1,0:T(1,128)S(1)}, f32[2,1024]{1,0:T(2,128)S(1)}) custom-call(f32[8]{0:T(128)} %weight_hbm.1, s32[2,1,2]{2,1,0:T(1,128)} %bitcast.9, s32[2,1,2]{2,1,0:T(1,128)} %bitcast.10, s32[1,2]{1,0:T(1,128)} %bitcast.11, bf16[16,16384]{1,0:T(8,128)(2,1)} %design_hbm.1, bf16[8,33]{1,0:T(8,128)(2,1)} %row_hbm.1, ...), custom_call_target="tpu_custom_call" | custom-call | tf_op jit(solution)/shard_map/pallas_call | solution.py:637
  24.3 0.8 %shard_map.92 = bf16[256,1024]{1,0:T(8,128)(2,1)} custom-call(f32[256,1024]{1,0:T(8,128)S(1)} %get-tuple-element.8.filtered, f32[1,1024]{1,0:T(1,128)S(1)} %get-tuple-element.9.mean, f32[2,1024]{1,0:T(2,128)S(1)} %get-tuple-element.10.scale), custom_call_target="tpu_custom_call" | custom-call | tf_op jit(solution)/shard_map/pallas_call | solution.py:699
